TPU v7x, 32 devices: a whole 2x2x4 slice. The times are simulated.
32 devices in a mesh: row: 4 (over y, core), col: 8 (over z, x).
Axes of the slice: x: 2, y: 2, z: 4, core: 2. Of those that a mesh axis runs over, the one named last changes fastest.
Arguments:
- tokens: bfloat16 [512, 8192], P('col', 'row'), may hold values from -6 to 6
- norm_gain: float32 [8192], P('row'), may hold values from 0.1 to 1.9
- gate_weight: bfloat16 [8192, 28672], P('row', 'col'), may hold values from -0.0625 to 0.0625
- up_weight: bfloat16 [8192, 28672], P('row', 'col'), may hold values from -0.0625 to 0.0625
- down_weight: bfloat16 [28672, 8192], P('col', 'row'), may hold values from -0.03125 to 0.03125
Outputs:
- block_out: bfloat16 [512, 8192], P('col', 'row')
All inputs are finite; a program needn't handle non-finite values.
Results may differ from a plain program's by a relative error of at most 0.0017.
Values may be sent and summed in bfloat16 or wider, within the bound.
A program may use at most 128 MiB of HBM per device.

v0:
```python
import jax
import jax.numpy as jnp
from jax import lax
from jax.sharding import PartitionSpec as P

D = 8192


epsilon = 1e-05


def local(tokens, norm_gain, gate_weight, up_weight, down_weight):
    gain_row = norm_gain.astype(jnp.float32)[None, :]
    gathered = lax.all_gather(tokens, "col", axis=0, tiled=True)
    values = gathered.astype(jnp.float32)
    squares = lax.psum(jnp.sum(values * values, axis=1), "row")
    normed = (values * lax.rsqrt(squares[:, None] / D + epsilon) * gain_row).astype(jnp.bfloat16)
    gate_part = jnp.dot(normed, gate_weight, preferred_element_type=jnp.float32)
    up_part = jnp.dot(normed, up_weight, preferred_element_type=jnp.float32)
    gate_sum, up_sum = (
        lax.psum_scatter(gate_part, "row", scatter_dimension=0, tiled=True),
        lax.psum_scatter(up_part, "row", scatter_dimension=0, tiled=True),
    )
    local_hidden = (jax.nn.silu(gate_sum) * up_sum).astype(jnp.bfloat16)
    hidden = lax.all_gather(local_hidden, "row", axis=0, tiled=True)

    def down_term(length):
        row_block = lax.slice_in_dim(hidden, 0, length, axis=0)
        return jnp.dot(row_block, down_weight, preferred_element_type=jnp.float32)

    branch_out = lax.psum_scatter(
        down_term(lax.axis_size("col") * tokens.shape[0]), "col", scatter_dimension=0, tiled=True
    )
    return (tokens.astype(jnp.float32) + branch_out).astype(jnp.bfloat16)


def solution(mesh):
    placed = (P("col", "row"), P("row"), P("row", "col"), P("row", "col"), P("col", "row"))
    return jax.shard_map(
        local, mesh=mesh, in_specs=placed, out_specs=P("col", "row"), check_vma=False
    )
```

profile of v0, /device:TPU:0, one launch (start us, length us, event | category | flops | bytes accessed | tf_op | source)
XLA Modules:
  0.0 361.8 jit_solution(13591276353215433253)
XLA Ops:
  6.5 0.0 all-gather.3.cloned.1.call-start
  6.5 0.7 all-gather.3.cloned.1.call-update
  7.3 0.0 reduce-scatter.6.cloned.1.call-start
  7.3 54.2 %all-gather.3.cloned.1.call-done = bf16[512,2048]{1,0:T(8,128)(2,1)} async-done(((bf16[64,2048]{1,0:T(8,128)(2,1)}), bf16[512,2048]{1,0:T(8,128)(2,1)}) %all-gather.3.cloned.1.call-update) | async-done | bytes 2097168 | tf_op jit(solution)/shard_map/all_gather | solution.py:14
  61.5 2.1 fusion
  63.6 5.7 %psum.7 = f32[512]{0:T(512)S(1)} all-reduce(f32[512]{0:T(512)S(1)} %fusion), channel_id=1, replica_groups=mesh['row'=4,'col'=8] {'row'}, use_global_device_ids=true, to_apply=%region_1.0 | all-reduce | flops 512 | bytes 4096 | tf_op jit(solution)/shard_map/psum | solution.py:16
  69.3 13.6 %fusion.3 = f32[512,3584]{1,0:T(8,128)} fusion(bf16[2048,3584]{1,0:T(8,128)(2,1)} %param.8, bf16[512,2048]{1,0:T(8,128)(2,1)} %all-gather.3.cloned.1.call-done, f32[2048]{0:T(1024)} %param.6, f32[512]{0:T(512)S(1)} %add_rsqrt_fusion), kind=kOutput, calls=%fused_computation.6 | convolution fusion | flops 7520387072 | bytes 24127488 | tf_op jit(solution)/shard_map/dot_general | solution.py:19
  82.9 0.0 copy-start
  82.9 0.0 copy-start.2
  82.9 0.0 reduce-scatter.6.cloned.1.call-update
  82.9 0.0 reduce-scatter.4.cloned.1.call-start
  83.0 1.5 copy-done
  84.5 0.0 copy-done.2
  84.5 13.1 %fusion.5 = f32[512,3584]{1,0:T(8,128)} fusion(bf16[2048,3584]{1,0:T(8,128)(2,1)} %param.7, bf16[512,2048]{1,0:T(8,128)(2,1)S(1)} %copy-done, f32[2048]{0:T(1024)S(1)} %copy-done.2, f32[512]{0:T(512)S(1)} %add_rsqrt_fusion), kind=kOutput, calls=%fused_computation.7 | convolution fusion | flops 7520387072 | bytes 24127488 | tf_op jit(solution)/shard_map/dot_general | solution.py:18
  97.6 0.0 reduce-scatter.4.cloned.1.call-update
  97.6 0.0 all-gather.5.cloned.1.call-start
  97.7 50.3 %reduce-scatter.6.cloned.1.call-done = f32[128,3584]{1,0:T(8,128)} async-done(((f32[512,3584]{1,0:T(8,128)}), f32[128,3584]{1,0:T(8,128)}) %reduce-scatter.6.cloned.1.call-update) | async-done | bytes 1835024 | tf_op jit(solution)/shard_map/reduce_scatter | solution.py:22
  148.0 68.4 %reduce-scatter.4.cloned.1.call-done = f32[128,3584]{1,0:T(8,128)} async-done(((f32[512,3584]{1,0:T(8,128)}), f32[128,3584]{1,0:T(8,128)}) %reduce-scatter.4.cloned.1.call-update) | async-done | bytes 1835024 | tf_op jit(solution)/shard_map/reduce_scatter | solution.py:21
  216.4 3.5 multiply_convert_fusion
  219.9 0.0 all-gather.5.cloned.1.call-update
  219.9 0.0 reduce-scatter.8.cloned.1.call-start
  220.0 31.5 %all-gather.5.cloned.1.call-done = bf16[512,3584]{1,0:T(8,128)(2,1)} async-done(((bf16[128,3584]{1,0:T(8,128)(2,1)}), bf16[512,3584]{1,0:T(8,128)(2,1)}) %all-gather.5.cloned.1.call-update) | async-done | bytes 3670032 | tf_op jit(solution)/shard_map/all_gather | solution.py:25
  251.5 13.4 %fusion.7 = f32[512,2048]{1,0:T(8,128)} fusion(bf16[512,3584]{1,0:T(8,128)(2,1)} %all-gather.5.cloned.1.call-done, bf16[3584,2048]{1,0:T(8,128)(2,1)} %param.9), kind=kOutput, calls=%fused_computation.10 | convolution fusion | flops 7516192768 | bytes 22544384 | tf_op jit(solution)/shard_map/dot_general | solution.py:29
  264.9 0.0 copy-start.1
  264.9 0.0 reduce-scatter.8.cloned.1.call-update
  264.9 88.5 %reduce-scatter.8.cloned.1.call-done = f32[64,2048]{1,0:T(8,128)} async-done(((f32[512,2048]{1,0:T(8,128)}), f32[64,2048]{1,0:T(8,128)}) %reduce-scatter.8.cloned.1.call-update) | async-done | bytes 524304 | tf_op jit(solution)/shard_map/reduce_scatter | solution.py:31
  353.4 0.0 copy-done.1
  353.4 1.8 add_convert_fusion
  (1 shorter events, 0.0 us)
Async XLA Ops:
  6.5 55.0 %all-gather.3.cloned.1.call-start = ((), (), s32[]{:S(2)}) async-start(), calls=%async_computation.3 | async-start | bytes 2359296 | tf_op jit(solution)/shard_map/all_gather | solution.py:14
  7.3 140.8 %reduce-scatter.6.cloned.1.call-start = ((), (), s32[]{:S(2)}) async-start(), calls=%async_computation.5 | async-start | bytes 9175040 | tf_op jit(solution)/shard_map/reduce_scatter | solution.py:22
  82.9 1.6 copy-start
  82.9 1.6 copy-start.2
  82.9 133.5 %reduce-scatter.4.cloned.1.call-start = ((), (), s32[]{:S(2)}) async-start(), calls=%async_computation.4 | async-start | bytes 9175040 | tf_op jit(solution)/shard_map/reduce_scatter | solution.py:21
  97.6 153.9 %all-gather.5.cloned.1.call-start = ((), (), s32[]{:S(2)}) async-start(), calls=%async_computation.6 | async-start | bytes 4587520 | tf_op jit(solution)/shard_map/all_gather | solution.py:25
  219.9 133.5 %reduce-scatter.8.cloned.1.call-start = ((), (), s32[]{:S(2)}) async-start(), calls=%async_computation.7 | async-start | bytes 4718592 | tf_op jit(solution)/shard_map/reduce_scatter | solution.py:31
  264.9 88.6 %copy-start.1 = (bf16[64,2048]{1,0:T(8,128)(2,1)S(1)}, bf16[64,2048]{1,0:T(8,128)(2,1)}, u32[]{:S(2)}) copy-start(bf16[64,2048]{1,0:T(8,128)(2,1)} %param.5) | copy-start | bytes 786436
Sparse Core Ops, SparseCore 0:
  9.5 52.0 all-gather.2
  83.0 64.9 reduce-scatter.5
  150.6 65.8 reduce-scatter.3
  220.1 31.3 all-gather.4
  265.0 88.3 reduce-scatter.7
where the time goes:
time: 362 us
  waiting for transfers between devices  294 us (81%)
  matrix products  40.1 us (11%)
  between operations  13.1 us (4%)
  other arithmetic  7.36 us (2%)
  blocking collectives  5.66 us (2%)
    reduce_scatter x1, waiting for transfers between devices, local(): lax.psum_scatter(down_term(lax.axis_size('col') * tokens.shape[0]), 'col'...  88.5 us
    reduce_scatter x1, waiting for transfers between devices, local(): lax.psum_scatter(gate_part, 'row', scatter_dimension=0, tiled=True)  68.4 us
    all_gather x1, waiting for transfers between devices, local(): gathered = lax.all_gather(tokens, 'col', axis=0, tiled=True)  54.2 us
    reduce_scatter x1, waiting for transfers between devices, local(): lax.psum_scatter(up_part, 'row', scatter_dimension=0, tiled=True)  50.3 us
    all_gather x1, waiting for transfers between devices, local(): hidden = lax.all_gather(local_hidden, 'row', axis=0, tiled=True)  31.5 us
    dot_general x1, matrix products, local(): up_part = jnp.dot(normed, up_weight, preferred_element_type=jnp.float32)  13.6 us
    dot_general x1, matrix products, down_term(): return jnp.dot(row_block, down_weight, preferred_element_type=jnp.float32)  13.4 us
    dot_general x1, matrix products, local(): gate_part = jnp.dot(normed, gate_weight, preferred_element_type=jnp.float32)  13.1 us
  transfers between devices with their start and end apart: 5, of which 5 were waited for; matrix products, arithmetic and copies ran while one was open for 4% of the time, Pallas kernels for 0%

commit v1 on v0

v1 whole, which is shorter than its diff:
```python
import functools

import jax
import jax.numpy as jnp
from jax import lax
from jax.experimental import pallas as pl
from jax.experimental.pallas import tpu as pltpu
from jax.sharding import PartitionSpec as P

MESH = pl.DeviceIdType.MESH
D = 8192
TILES = 7
CORES = 2
PASSES = 2
VMEM_LIMIT = 67043328


epsilon = 1e-05


def block_kernel(
    rows, xs, zs,
    tokens, gain, gate_hbm, up_hbm, down_hbm, out,
    squares_out, squares_in, normed, gate_buf, up_buf, down_buf, part, from_core, sums_out, sums_in, hid,
    acc, x_in, z_out, z_in,
    s_send, s_recv, ga_send, ga_recv, gb_send, gb_recv, w_sem, d_sem, core_send, core_recv, y_send, y_recv,
    h_send, h_recv, p_send, p_recv, rx_send, rx_recv, rz_send, rz_recv,
):
    chips = rows // CORES
    me = lax.axis_index("row")
    y, core = me // CORES, me % CORES
    partner = y * CORES + (1 - core)
    at = lax.axis_index("col")
    z, x = at // xs, at % xs
    count = tokens.shape[0]
    piece = count // PASSES
    line = zs * piece
    span = normed.shape[1]
    half, block = span // CORES, span // rows
    width = gate_buf.shape[2]
    total_steps = PASSES * TILES

    def remote(src, dst, send, recv, device):
        return pltpu.make_async_remote_copy(src, dst, send, recv, device_id=device, device_id_type=MESH)

    def peer(d):
        return lax.rem(y + d, chips)

    def z_peer(d):
        return {"col": lax.rem(z + d, zs) * xs + x}

    def x_peer(e):
        return {"col": z * xs + lax.rem(x + e, xs)}

    def spot(to_x, to_z):
        return pl.ds(pl.multiple_of(to_x * line + to_z * piece, piece), piece)

    def line_of(to_x):
        return pl.ds(pl.multiple_of(to_x * line, line), line)

    def mine(chip):
        return pl.ds(pl.multiple_of(core * half + chip * block, block), block)

    def weights(u):
        slot = lax.rem(u, 2)
        columns = pl.ds(pl.multiple_of(lax.rem(u, TILES) * width, width), width)
        return (
            pltpu.make_async_copy(gate_hbm.at[:, columns], gate_buf.at[slot], w_sem.at[slot, 0]),
            pltpu.make_async_copy(up_hbm.at[:, columns], up_buf.at[slot], w_sem.at[slot, 1]),
        )

    def down_weights(u):
        slot = lax.rem(u, 2)
        lines = pl.ds(pl.multiple_of(lax.rem(u, TILES) * width, width), width)
        return pltpu.make_async_copy(down_hbm.at[lines, :], down_buf.at[slot], d_sem.at[slot])

    def s_copy(d):
        return remote(squares_out, squares_in.at[d - 1], s_send.at[d - 1], s_recv.at[d - 1],
                      {"row": lax.rem(me + d, rows)})

    def ga_copy(p, d):
        return remote(normed.at[p, spot(x, z)], normed.at[p, spot(x, z)],
                      ga_send.at[p, d - 1], ga_recv.at[p, d - 1], z_peer(d))

    def gb_copy(p, e):
        return remote(normed.at[p, line_of(x)], normed.at[p, line_of(x)],
                      gb_send.at[p, e - 1], gb_recv.at[p, e - 1], x_peer(e))

    def rx_copy(p, e):
        return remote(acc.at[p, line_of(lax.rem(x + e, xs))], x_in.at[p, e - 1],
                      rx_send.at[p, e - 1], rx_recv.at[p, e - 1], x_peer(e))

    def rz_copy(p, d):
        return remote(z_out.at[p, d - 1], z_in.at[p, d - 1],
                      rz_send.at[p, d - 1], rz_recv.at[p, d - 1], z_peer(d))

    def core_copy(u):
        other = pl.ds(pl.multiple_of((1 - core) * half, half), half)
        return remote(part.at[u, other], from_core.at[u], core_send.at[u], core_recv.at[u], {"row": partner})

    def y_copy(u, d):
        return remote(sums_out.at[u, d - 1], sums_in.at[u, d - 1], y_send.at[u, d - 1], y_recv.at[u, d - 1],
                      {"row": peer(d) * CORES + core})

    def h_copy(u, d):
        return remote(hid.at[u, mine(y)], hid.at[u, mine(y)], h_send.at[u, d - 1], h_recv.at[u, d - 1],
                      {"row": peer(d) * CORES + core})

    def p_copy(u, d):
        source = lax.rem(y + chips - d, chips)
        return remote(hid.at[u, mine(source)], hid.at[u, mine(source)], p_send.at[u, d], p_recv.at[u, d],
                      {"row": partner})

    for copy in weights(0):
        copy.start()
    down_weights(0).start()

    values = tokens[...].astype(jnp.float32)
    own_squares = jnp.sum(values * values, axis=1, keepdims=True)
    squares_out[...] = jnp.broadcast_to(own_squares, squares_out.shape)

    barrier = pltpu.get_barrier_semaphore()
    for d in range(1, rows):
        pl.semaphore_signal(barrier, inc=1, device_id={"row": lax.rem(me + d, rows)}, device_id_type=MESH)
    for d in range(1, zs):
        pl.semaphore_signal(barrier, inc=1, device_id=z_peer(d), device_id_type=MESH)
    for e in range(1, xs):
        pl.semaphore_signal(barrier, inc=1, device_id=x_peer(e), device_id_type=MESH)
    pl.semaphore_wait(barrier, rows + zs + xs - 3)

    for d in range(1, rows):
        s_copy(d).start()
    squares = squares_out[...]
    for d in range(1, rows):
        s_copy(d).wait_recv()
        squares += squares_in[d - 1]
    factor = lax.rsqrt(squares[:, :1] / D + epsilon)
    scaled = (values * factor * gain[...]).astype(jnp.bfloat16)

    def gather_z(p):
        for d in range(1, zs):
            ga_copy(p, d).start()

    def gather_x(p):
        for d in range(1, zs):
            ga_copy(p, d).wait_recv()
        for e in range(1, xs):
            gb_copy(p, e).start()

    def gather_end(p):
        for e in range(1, xs):
            gb_copy(p, e).wait_recv()

    def scatter_x(p):
        for e in range(1, xs):
            rx_copy(p, e).start()

    def line_sum(p, to_z):
        value = acc[p, spot(x, to_z), :]
        near = pl.ds(pl.multiple_of(to_z * piece, piece), piece)
        for e in range(1, xs):
            value += x_in[p, e - 1, near, :]
        return value

    def scatter_z(p):
        for e in range(1, xs):
            rx_copy(p, e).wait_recv()
        for d in range(1, zs):
            z_out[p, d - 1, :, :] = line_sum(p, lax.rem(z + d, zs))
            rz_copy(p, d).start()

    def scatter_end(p):
        value = line_sum(p, z)
        for d in range(1, zs):
            rz_copy(p, d).wait_recv()
            value += z_in[p, d - 1, :, :]
        here = pl.ds(p * piece, piece)
        out[here, :] = (tokens[here, :].astype(jnp.float32) + value).astype(out.dtype)

    for p in range(PASSES):
        normed[p, spot(x, z), :] = scaled[p * piece:(p + 1) * piece]
    gather_z(0)
    gather_x(0)
    gather_end(0)

    def chip_sum(u, chip):
        near = pl.ds(pl.multiple_of(chip * block, block), block)
        return part[u, mine(chip), :] + from_core[u, near, :]

    def step(j, carry):
        for p in range(1, PASSES):
            first = (p - 1) * TILES
            pl.when(j == first)(functools.partial(gather_z, p))
            pl.when(j == first + 4)(functools.partial(gather_x, p))
            pl.when(j == first + TILES)(functools.partial(gather_end, p))

        @pl.when(j < total_steps)
        def _():
            for copy in weights(j):
                copy.wait()

            @pl.when(j + 1 < total_steps)
            def _():
                for copy in weights(j + 1):
                    copy.start()

            slot, p = lax.rem(j, 2), j // TILES
            part[j, :, :width] = jnp.dot(normed[p], gate_buf[slot], preferred_element_type=jnp.float32)
            part[j, :, width:] = jnp.dot(normed[p], up_buf[slot], preferred_element_type=jnp.float32)
            core_copy(j).start()

        @pl.when((j >= 1) & (j < total_steps + 1))
        def _():
            u = j - 1
            core_copy(u).wait_recv()
            for d in range(1, chips):
                sums_out[u, d - 1, :, :] = chip_sum(u, peer(d))
                y_copy(u, d).start()

        @pl.when((j >= 2) & (j < total_steps + 2))
        def _():
            u = j - 2
            total = chip_sum(u, y)
            for d in range(1, chips):
                y_copy(u, d).wait_recv()
                total += sums_in[u, d - 1, :, :]
            hid[u, mine(y), :] = (jax.nn.silu(total[:, :width]) * total[:, width:]).astype(jnp.bfloat16)
            for d in range(1, chips):
                h_copy(u, d).start()
            p_copy(u, 0).start()

        @pl.when((j >= 3) & (j < total_steps + 3))
        def _():
            u = j - 3
            for d in range(1, chips):
                h_copy(u, d).wait_recv()
                p_copy(u, d).start()

        @pl.when(j >= 4)
        def _():
            u = j - 4
            p, t = u // TILES, lax.rem(u, TILES)
            down_weights(u).wait()

            @pl.when(u + 1 < total_steps)
            def _():
                down_weights(u + 1).start()

            for d in range(chips):
                p_copy(u, d).wait_recv()
            term = jnp.dot(hid[u], down_buf[lax.rem(u, 2)], preferred_element_type=jnp.float32)

            @pl.when(t == 0)
            def _():
                acc[p, :, :] = term

            @pl.when(t > 0)
            def _():
                acc[p, :, :] += term

        for p in range(PASSES - 1):
            last = (p + 1) * TILES + 3
            pl.when(j == last)(functools.partial(scatter_x, p))
            pl.when(j == last + 4)(functools.partial(scatter_z, p))
            pl.when(j == last + 7)(functools.partial(scatter_end, p))
        return carry

    lax.fori_loop(0, total_steps + 4, step, 0)

    scatter_x(PASSES - 1)
    scatter_z(PASSES - 1)
    scatter_end(PASSES - 1)

    for d in range(1, rows):
        s_copy(d).wait_send()
    for p in range(PASSES):
        for d in range(1, zs):
            ga_copy(p, d).wait_send()
            rz_copy(p, d).wait_send()
        for e in range(1, xs):
            gb_copy(p, e).wait_send()
            rx_copy(p, e).wait_send()

    def drain(u, carry):
        core_copy(u).wait_send()
        for d in range(1, chips):
            y_copy(u, d).wait_send()
            h_copy(u, d).wait_send()
        for d in range(chips):
            p_copy(u, d).wait_send()
        return carry

    lax.fori_loop(0, total_steps, drain, 0)


def local(tokens, norm_gain, gate_weight, up_weight, down_weight):
    rows, cols = lax.axis_size("row"), lax.axis_size("col")
    xs = max(x for x in range(1, cols + 1) if cols % x == 0 and x * x <= cols)
    zs = cols // xs
    count, depth = tokens.shape
    hidden, features = down_weight.shape
    width, piece = hidden // TILES, count // PASSES
    span, chips = cols * piece, rows // CORES
    half, block = span // CORES, span // rows
    steps = PASSES * TILES
    hbm = pl.BlockSpec(memory_space=pl.ANY)
    vmem = pl.BlockSpec(memory_space=pltpu.VMEM)
    dma = pltpu.SemaphoreType.DMA
    f32, bf16 = jnp.float32, jnp.bfloat16
    return pl.pallas_call(
        functools.partial(block_kernel, rows, xs, zs),
        out_shape=jax.ShapeDtypeStruct((count, features), bf16),
        in_specs=[vmem, vmem, hbm, hbm, hbm],
        out_specs=vmem,
        scratch_shapes=[
            pltpu.VMEM((count, 128), f32),
            pltpu.VMEM((rows - 1, count, 128), f32),
            pltpu.VMEM((PASSES, span, depth), bf16),
            pltpu.VMEM((2, depth, width), bf16),
            pltpu.VMEM((2, depth, width), bf16),
            pltpu.VMEM((2, width, features), bf16),
            pltpu.VMEM((steps, span, 2 * width), f32),
            pltpu.VMEM((steps, half, 2 * width), f32),
            pltpu.VMEM((steps, chips - 1, block, 2 * width), f32),
            pltpu.VMEM((steps, chips - 1, block, 2 * width), f32),
            pltpu.VMEM((steps, span, width), bf16),
            pltpu.VMEM((PASSES, span, features), f32),
            pltpu.VMEM((PASSES, xs - 1, zs * piece, features), f32),
            pltpu.VMEM((PASSES, zs - 1, piece, features), f32),
            pltpu.VMEM((PASSES, zs - 1, piece, features), f32),
            dma((rows - 1,)), dma((rows - 1,)),
            dma((PASSES, zs - 1)), dma((PASSES, zs - 1)),
            dma((PASSES, xs - 1)), dma((PASSES, xs - 1)),
            dma((2, 2)), dma((2,)),
            dma((steps,)), dma((steps,)),
            dma((steps, chips - 1)), dma((steps, chips - 1)),
            dma((steps, chips - 1)), dma((steps, chips - 1)),
            dma((steps, chips)), dma((steps, chips)),
            dma((PASSES, xs - 1)), dma((PASSES, xs - 1)),
            dma((PASSES, zs - 1)), dma((PASSES, zs - 1)),
        ],
        compiler_params=pltpu.CompilerParams(
            collective_id=1, has_side_effects=True, vmem_limit_bytes=VMEM_LIMIT),
        name="block",
    )(tokens, norm_gain[None, :], gate_weight, up_weight, down_weight)


def solution(mesh):
    placed = (P("col", "row"), P("row"), P("row", "col"), P("row", "col"), P("col", "row"))
    return jax.shard_map(
        local, mesh=mesh, in_specs=placed, out_specs=P("col", "row"), check_vma=False
    )
```

time: 362 us -> 196 us (0.54)
  the two profiles are of different devices: /device:TPU:0 before, /device:TPU:22 now
where the time goes in v1:
time: 196 us; the launch traced here: 195 us
  Pallas kernels  194 us (99%)
    pallas_call x1, Pallas kernels, local(): pl.pallas_call(functools.partial(block_kernel, rows, xs, zs), out_shape=j...  194 us

profile of v1, /device:TPU:22, one launch (start us, length us, event | category | flops | bytes accessed | tf_op | source)
XLA Modules:
  0.0 195.3 jit_solution(15690837293402631843)
XLA Ops:
  0.0 193.6 %block.1 = bf16[64,2048]{1,0:T(8,128)(2,1)} custom-call(bf16[64,2048]{1,0:T(8,128)(2,1)} %tokens.1, f32[1,2048]{1,0:T(1,128)} %bitcast.1, bf16[2048,3584]{1,0:T(8,128)(2,1)} %gate_hbm.1, bf16[2048,3584]{1,0:T(8,128)(2,1)} %up_hbm.1, bf16[3584,2048]{1,0:T(8,128)(2,1)} %down_hbm.1), custom_call_target="tpu_custom_call" | custom-call | tf_op jit(solution)/shard_map/block/pallas_call | solution.py:310
  193.6 1.7 copy.7

commit v2 on v1

--- a/solution.py
+++ b/solution.py
@@ -11,7 +11,8 @@
 D = 8192
 TILES = 7
 CORES = 2
-PASSES = 2
+PASSES = 4
+LAG = 3
 VMEM_LIMIT = 67043328
 
 
@@ -55,9 +56,6 @@
     def spot(to_x, to_z):
         return pl.ds(pl.multiple_of(to_x * line + to_z * piece, piece), piece)
 
-    def line_of(to_x):
-        return pl.ds(pl.multiple_of(to_x * line, line), line)
-
     def mine(chip):
         return pl.ds(pl.multiple_of(core * half + chip * block, block), block)
 
@@ -82,13 +80,16 @@
         return remote(normed.at[p, spot(x, z)], normed.at[p, spot(x, z)],
                       ga_send.at[p, d - 1], ga_recv.at[p, d - 1], z_peer(d))
 
-    def gb_copy(p, e):
-        return remote(normed.at[p, line_of(x)], normed.at[p, line_of(x)],
-                      gb_send.at[p, e - 1], gb_recv.at[p, e - 1], x_peer(e))
-
-    def rx_copy(p, e):
-        return remote(acc.at[p, line_of(lax.rem(x + e, xs))], x_in.at[p, e - 1],
-                      rx_send.at[p, e - 1], rx_recv.at[p, e - 1], x_peer(e))
+    def gb_copy(p, e, d):
+        here = spot(x, lax.rem(z + zs - d, zs))
+        return remote(normed.at[p, here], normed.at[p, here],
+                      gb_send.at[p, e - 1, d], gb_recv.at[p, e - 1, d], x_peer(e))
+
+    def rx_copy(p, e, d):
+        to_z = lax.rem(z + d, zs)
+        near = pl.ds(pl.multiple_of(to_z * piece, piece), piece)
+        return remote(acc.at[p, spot(lax.rem(x + e, xs), to_z)], x_in.at[p, e - 1, near],
+                      rx_send.at[p, e - 1, d], rx_recv.at[p, e - 1, d], x_peer(e))
 
     def rz_copy(p, d):
         return remote(z_out.at[p, d - 1], z_in.at[p, d - 1],
@@ -142,18 +143,21 @@
             ga_copy(p, d).start()
 
     def gather_x(p):
-        for d in range(1, zs):
-            ga_copy(p, d).wait_recv()
-        for e in range(1, xs):
-            gb_copy(p, e).start()
+        for d in range(zs):
+            if d:
+                ga_copy(p, d).wait_recv()
+            for e in range(1, xs):
+                gb_copy(p, e, d).start()
 
     def gather_end(p):
-        for e in range(1, xs):
-            gb_copy(p, e).wait_recv()
+        for d in range(zs):
+            for e in range(1, xs):
+                gb_copy(p, e, d).wait_recv()
 
     def scatter_x(p):
-        for e in range(1, xs):
-            rx_copy(p, e).start()
+        for d in (*range(1, zs), 0):
+            for e in range(1, xs):
+                rx_copy(p, e, d).start()
 
     def line_sum(p, to_z):
         value = acc[p, spot(x, to_z), :]
@@ -163,13 +167,15 @@
         return value
 
     def scatter_z(p):
-        for e in range(1, xs):
-            rx_copy(p, e).wait_recv()
         for d in range(1, zs):
+            for e in range(1, xs):
+                rx_copy(p, e, d).wait_recv()
             z_out[p, d - 1, :, :] = line_sum(p, lax.rem(z + d, zs))
             rz_copy(p, d).start()
 
     def scatter_end(p):
+        for e in range(1, xs):
+            rx_copy(p, e, 0).wait_recv()
         value = line_sum(p, z)
         for d in range(1, zs):
             rz_copy(p, d).wait_recv()
@@ -191,7 +197,7 @@
         for p in range(1, PASSES):
             first = (p - 1) * TILES
             pl.when(j == first)(functools.partial(gather_z, p))
-            pl.when(j == first + 4)(functools.partial(gather_x, p))
+            pl.when(j == first + 3)(functools.partial(gather_x, p))
             pl.when(j == first + TILES)(functools.partial(gather_end, p))
 
         @pl.when(j < total_steps)
@@ -217,9 +223,9 @@
                 sums_out[u, d - 1, :, :] = chip_sum(u, peer(d))
                 y_copy(u, d).start()
 
-        @pl.when((j >= 2) & (j < total_steps + 2))
-        def _():
-            u = j - 2
+        @pl.when((j >= LAG) & (j < total_steps + LAG))
+        def _():
+            u = j - LAG
             total = chip_sum(u, y)
             for d in range(1, chips):
                 y_copy(u, d).wait_recv()
@@ -229,16 +235,16 @@
                 h_copy(u, d).start()
             p_copy(u, 0).start()
 
-        @pl.when((j >= 3) & (j < total_steps + 3))
-        def _():
-            u = j - 3
+        @pl.when((j >= LAG + 1) & (j < total_steps + LAG + 1))
+        def _():
+            u = j - LAG - 1
             for d in range(1, chips):
                 h_copy(u, d).wait_recv()
                 p_copy(u, d).start()
 
-        @pl.when(j >= 4)
-        def _():
-            u = j - 4
+        @pl.when(j >= LAG + 2)
+        def _():
+            u = j - LAG - 2
             p, t = u // TILES, lax.rem(u, TILES)
             down_weights(u).wait()
 
@@ -259,15 +265,17 @@
                 acc[p, :, :] += term
 
         for p in range(PASSES - 1):
-            last = (p + 1) * TILES + 3
+            last = (p + 1) * TILES + LAG + 1
             pl.when(j == last)(functools.partial(scatter_x, p))
             pl.when(j == last + 4)(functools.partial(scatter_z, p))
-            pl.when(j == last + 7)(functools.partial(scatter_end, p))
+            if p < PASSES - 2:
+                pl.when(j == last + 10)(functools.partial(scatter_end, p))
         return carry
 
-    lax.fori_loop(0, total_steps + 4, step, 0)
+    lax.fori_loop(0, total_steps + LAG + 2, step, 0)
 
     scatter_x(PASSES - 1)
+    scatter_end(PASSES - 2)
     scatter_z(PASSES - 1)
     scatter_end(PASSES - 1)
 
@@ -278,8 +286,9 @@
             ga_copy(p, d).wait_send()
             rz_copy(p, d).wait_send()
         for e in range(1, xs):
-            gb_copy(p, e).wait_send()
-            rx_copy(p, e).wait_send()
+            for d in range(zs):
+                gb_copy(p, e, d).wait_send()
+                rx_copy(p, e, d).wait_send()
 
     def drain(u, carry):
         core_copy(u).wait_send()
@@ -330,13 +339,13 @@
             pltpu.VMEM((PASSES, zs - 1, piece, features), f32),
             dma((rows - 1,)), dma((rows - 1,)),
             dma((PASSES, zs - 1)), dma((PASSES, zs - 1)),
-            dma((PASSES, xs - 1)), dma((PASSES, xs - 1)),
+            dma((PASSES, xs - 1, zs)), dma((PASSES, xs - 1, zs)),
             dma((2, 2)), dma((2,)),
             dma((steps,)), dma((steps,)),
             dma((steps, chips - 1)), dma((steps, chips - 1)),
             dma((steps, chips - 1)), dma((steps, chips - 1)),
             dma((steps, chips)), dma((steps, chips)),
-            dma((PASSES, xs - 1)), dma((PASSES, xs - 1)),
+            dma((PASSES, xs - 1, zs)), dma((PASSES, xs - 1, zs)),
             dma((PASSES, zs - 1)), dma((PASSES, zs - 1)),
         ],
         compiler_params=pltpu.CompilerParams(

time: 196 us -> 152 us (0.78)
  the two profiles are of different devices: /device:TPU:22 before, /device:TPU:0 now
where the time goes in v2:
time: 152 us
  Pallas kernels  150 us (99%)
  local copies, waits for them, and re-layouts  1.67 us (1%)
    pallas_call x1, Pallas kernels, local(): pl.pallas_call(functools.partial(block_kernel, rows, xs, zs), out_shape=j...  150 us

profile of v2, /device:TPU:0, one launch (start us, length us, event | category | flops | bytes accessed | tf_op | source)
XLA Modules:
  0.0 152.1 jit_solution(5104179247323826503)
XLA Ops:
  0.0 150.4 %block.1 = bf16[64,2048]{1,0:T(8,128)(2,1)} custom-call(bf16[64,2048]{1,0:T(8,128)(2,1)} %tokens.1, f32[1,2048]{1,0:T(1,128)} %bitcast.1, bf16[2048,3584]{1,0:T(8,128)(2,1)} %gate_hbm.1, bf16[2048,3584]{1,0:T(8,128)(2,1)} %up_hbm.1, bf16[3584,2048]{1,0:T(8,128)(2,1)} %down_hbm.1), custom_call_target="tpu_custom_call" | custom-call | tf_op jit(solution)/shard_map/block/pallas_call | solution.py:319
  150.4 1.7 %copy.7 = bf16[64,2048]{1,0:T(8,128)(2,1)} copy(bf16[64,2048]{1,0:T(8,128)(2,1)} %block.1) | data formatting | bytes 524288

commit v3 on v2

--- a/solution.py
+++ b/solution.py
@@ -235,16 +235,16 @@
                 h_copy(u, d).start()
             p_copy(u, 0).start()
 
-        @pl.when((j >= LAG + 1) & (j < total_steps + LAG + 1))
-        def _():
-            u = j - LAG - 1
+        @pl.when((j >= LAG + 2) & (j < total_steps + LAG + 2))
+        def _():
+            u = j - LAG - 2
             for d in range(1, chips):
                 h_copy(u, d).wait_recv()
                 p_copy(u, d).start()
 
-        @pl.when(j >= LAG + 2)
-        def _():
-            u = j - LAG - 2
+        @pl.when(j >= LAG + 3)
+        def _():
+            u = j - LAG - 3
             p, t = u // TILES, lax.rem(u, TILES)
             down_weights(u).wait()
 
@@ -265,14 +265,14 @@
                 acc[p, :, :] += term
 
         for p in range(PASSES - 1):
-            last = (p + 1) * TILES + LAG + 1
+            last = (p + 1) * TILES + LAG + 2
             pl.when(j == last)(functools.partial(scatter_x, p))
             pl.when(j == last + 4)(functools.partial(scatter_z, p))
             if p < PASSES - 2:
                 pl.when(j == last + 10)(functools.partial(scatter_end, p))
         return carry
 
-    lax.fori_loop(0, total_steps + LAG + 2, step, 0)
+    lax.fori_loop(0, total_steps + LAG + 3, step, 0)
 
     scatter_x(PASSES - 1)
     scatter_end(PASSES - 2)

time: 152 us -> 151 us (level)
  no operation moved by 1% of the time
where the time goes in v3:
time: 151 us
  Pallas kernels  149 us (99%)
  local copies, waits for them, and re-layouts  1.67 us (1%)
    pallas_call x1, Pallas kernels, local(): pl.pallas_call(functools.partial(block_kernel, rows, xs, zs), out_shape=j...  149 us

profile of v3, /device:TPU:0, one launch (start us, length us, event | category | flops | bytes accessed | tf_op | source)
XLA Modules:
  0.0 150.9 jit_solution(2572241714553980541)
XLA Ops:
  0.0 149.3 %block.1 = bf16[64,2048]{1,0:T(8,128)(2,1)} custom-call(bf16[64,2048]{1,0:T(8,128)(2,1)} %tokens.1, f32[1,2048]{1,0:T(1,128)} %bitcast.1, bf16[2048,3584]{1,0:T(8,128)(2,1)} %gate_hbm.1, bf16[2048,3584]{1,0:T(8,128)(2,1)} %up_hbm.1, bf16[3584,2048]{1,0:T(8,128)(2,1)} %down_hbm.1), custom_call_target="tpu_custom_call" | custom-call | tf_op jit(solution)/shard_map/block/pallas_call | solution.py:319
  149.3 1.7 %copy.7 = bf16[64,2048]{1,0:T(8,128)(2,1)} copy(bf16[64,2048]{1,0:T(8,128)(2,1)} %block.1) | data formatting | bytes 524288
